TPU v7x, 16 devices: a whole 2x2x2 slice. The times are simulated.
16 devices in a mesh: dp: 1, tp: 16 (over x, y, z, core).
Axes of the slice: x: 2, y: 2, z: 2, core: 2. Of those that a mesh axis runs over, the one named last changes fastest.
Arguments:
- x: bfloat16 [64, 2048], P('dp')
- k_cache: bfloat16 [64, 4096, 16, 128], P('dp', None, 'tp')
- v_cache: bfloat16 [64, 4096, 16, 128], P('dp', None, 'tp')
- gain_a: bfloat16 [2048], replicated
- wq: bfloat16 [2048, 2048], P(None, 'tp')
- wo: bfloat16 [2048, 2048], P('tp')
- gain_m: bfloat16 [2048], replicated
- w_gate: bfloat16 [2048, 8192], P(None, 'tp')
- w_up: bfloat16 [2048, 8192], P(None, 'tp')
- w_down: bfloat16 [8192, 2048], P('tp')
Outputs:
- output: bfloat16 [64, 2048], P('dp')
All inputs are finite; a program needn't handle non-finite values.
Results may differ from a plain program's by a relative error of at most 0.017.
Values are sent between devices in bfloat16 or wider.
A program may use at most 2 GiB of HBM per device.

v0:
```python
import jax
import jax.numpy as jnp
from jax import lax
from jax.sharding import PartitionSpec as P

HEAD = 128
THETA = 10000


def normed(x, gain):
    wide = x.astype(jnp.float32)
    scale = lax.rsqrt(jnp.mean(wide * wide, -1, keepdims=True) + 1e-6)
    return (wide * scale * gain.astype(jnp.float32)).astype(jnp.bfloat16)


def turned(t, place, theta):
    half = t.shape[-1] // 2
    angle = place.astype(jnp.float32)[:, None] * theta ** (-jnp.arange(half, dtype=jnp.float32) / half)
    cos, sin = jnp.cos(angle)[:, None], jnp.sin(angle)[:, None]
    a, b = t[..., :half].astype(jnp.float32), t[..., half:].astype(jnp.float32)
    return jnp.concatenate([a * cos - b * sin, b * cos + a * sin], -1).astype(jnp.bfloat16)


def matmul(a, w):
    return jnp.dot(a, w, preferred_element_type=jnp.float32).astype(jnp.bfloat16)


def einsum(form, a, b):
    return jnp.einsum(form, a.astype(jnp.float32), b.astype(jnp.float32))


def seen_by(a, wq, k_cache, v_cache, head, theta):
    batch, cache, kv_heads = k_cache.shape[:3]
    place = jnp.full((batch,), cache - 1)
    q = turned(matmul(a, wq).reshape(batch, -1, head), place, theta).reshape(batch, kv_heads, -1, head)
    scores = einsum("bgsd,bugd->bgsu", q, k_cache) * head**-0.5
    weights = jax.nn.softmax(scores, -1).astype(jnp.bfloat16)
    return einsum("bgsu,bugd->bgsd", weights, v_cache).astype(jnp.bfloat16).reshape(batch, -1)


def hidden_of(b, w_gate, w_up):
    gate = jnp.dot(b, w_gate, preferred_element_type=jnp.float32)
    up = jnp.dot(b, w_up, preferred_element_type=jnp.float32)
    return (jax.nn.silu(gate) * up).astype(jnp.bfloat16)


def solution(mesh):
    def added(t, term):
        return (t.astype(jnp.float32) + lax.psum(term.astype(jnp.bfloat16), "tp").astype(jnp.float32)).astype(jnp.bfloat16)

    def step(x, k_cache, v_cache, gain_a, wq, wo, gain_m, w_gate, w_up, w_down):
        seen = seen_by(normed(x, gain_a), wq, k_cache, v_cache, HEAD, THETA)
        h = added(x, jnp.dot(seen, wo, preferred_element_type=jnp.float32))
        return added(h, jnp.dot(hidden_of(normed(h, gain_m), w_gate, w_up), w_down, preferred_element_type=jnp.float32))

    states, cache, columns, rows_of = P("dp", None), P("dp", None, "tp", None), P(None, "tp"), P("tp", None)
    return jax.shard_map(
        step,
        mesh=mesh,
        in_specs=(states, cache, cache, P(None), columns, rows_of, P(None), columns, columns, rows_of),
        out_specs=states,
        check_vma=False,
    )
```

profile of v0, /device:TPU:0, one launch (start us, length us, event | category | flops | bytes accessed | tf_op | source)
XLA Modules:
  0.0 209.0 jit_solution(9636945289684125330)
XLA Ops:
  6.5 0.0 copy-start
  6.5 0.0 all-reduce.3.cloned.1.call-start
  6.6 0.8 convert_element_type.68
  7.4 1.1 fusion.9
  8.5 1.4 fusion.5
  10.0 0.1 fusion.37
  10.0 0.1 maximum_bitcast_fusion
  10.1 25.3 %fusion.2 = f32[64,1,4096]{2,1,0:T(1,128)S(1)} fusion(bf16[64,4096,1,128]{3,1,2,0:T(8,128)(2,1)} %param.11, bf16[64,128,1]{1,0,2:T(8,128)(2,1)S(1)} %maximum_bitcast_fusion), kind=kOutput, calls=%fused_computation.2 | convolution fusion | flops 67108864 | bytes 68173824 | tf_op jit(solution)/shard_map/bgsd,bugd->bgsu/dot_general | solution.py:29
  35.5 0.8 fusion.8
  36.2 0.8 fusion.7
  37.0 0.8 fusion.17
  37.9 0.0 copy-start.2
  37.9 0.0 copy-start.3
  37.9 0.0 copy-start.1
  37.9 22.7 %fusion = f32[64,1,128]{2,1,0:T(1,128)S(1)} fusion(bf16[64,4096,1,128]{3,1,2,0:T(8,128)(2,1)} %param.12, bf16[64,4096,1]{1,0,2:T(8,128)(2,1)S(1)} %fusion.17), kind=kOutput, calls=%fused_computation | convolution fusion | flops 67108864 | bytes 67665920 | tf_op jit(solution)/shard_map/bgsu,bugd->bgsd/dot_general | solution.py:29
  60.6 0.0 copy-done.2
  60.6 0.9 convolution_convert_fusion.1
  61.6 0.0 all-reduce.3.cloned.1.call-update
  61.6 0.0 all-reduce.5.cloned.1.call-start
  61.6 0.0 copy-done.3
  61.7 68.2 %all-reduce.3.cloned.1.call-done = bf16[64,2048]{1,0:T(8,128)(2,1)} async-done(((bf16[64,2048]{1,0:T(8,128)(2,1)}), bf16[64,2048]{1,0:T(8,128)(2,1)}) %all-reduce.3.cloned.1.call-update) | async-done | bytes 262160 | tf_op jit(solution)/shard_map/psum | solution.py:49
  129.9 0.0 copy-done.1
  129.9 1.1 fusion.13
  131.0 2.1 %fusion.28 = f32[64,512]{1,0:T(8,128)S(1)} fusion(bf16[2048,512]{1,0:T(8,128)(2,1)} %param.17, bf16[64,2048]{1,0:T(8,128)(2,1)S(1)} %get-tuple-element.6, f32[2048]{0:T(1024)S(1)} %convert_element_type.79, f32[64]{0:T(128)S(1)} %add_rsqrt_fusion), kind=kOutput, calls=%fused_computation.38 | convolution fusion | flops 134742016 | bytes 2498816 | tf_op jit(solution)/shard_map/dot_general | solution.py:42
  133.2 0.0 copy-done
  133.2 3.3 %convolution_convert_fusion = bf16[64,2048]{1,0:T(8,128)(2,1)} fusion(bf16[512,2048]{1,0:T(8,128)(2,1)S(1)} %copy-done, bf16[2048,512]{1,0:T(8,128)(2,1)} %param.18, f32[64,512]{1,0:T(8,128)S(1)} %fusion.28, bf16[64,2048]{1,0:T(8,128)(2,1)S(1)} %get-tuple-element.6, f32[2048]{0:T(1024)S(1)} %convert_element_type.79, f32[64]{0:T(128)S(1)} %add_rsqrt_fusion), kind=kOutput, calls=%fused_computation.4 | convolution fusion | flops 269287424 | bytes 4858112 | tf_op jit(solution)/shard_map/dot_general | solution.py:54
  136.4 0.0 all-reduce.5.cloned.1.call-update
  136.5 64.0 %all-reduce.5.cloned.1.call-done = bf16[64,2048]{1,0:T(8,128)(2,1)} async-done(((bf16[64,2048]{1,0:T(8,128)(2,1)}), bf16[64,2048]{1,0:T(8,128)(2,1)}) %all-reduce.5.cloned.1.call-update) | async-done | bytes 262160 | tf_op jit(solution)/shard_map/psum | solution.py:49
  200.4 1.7 fusion.16
  (4 shorter events, 0.1 us)
Async XLA Ops:
  6.5 126.6 %copy-start = (bf16[512,2048]{1,0:T(8,128)(2,1)S(1)}, bf16[512,2048]{1,0:T(8,128)(2,1)}, u32[]{:S(2)}) copy-start(bf16[512,2048]{1,0:T(8,128)(2,1)} %param.19) | copy-start | bytes 6291460
  6.5 123.3 %all-reduce.3.cloned.1.call-start = ((), (), s32[]{:S(2)}) async-start(), calls=%async_computation | async-start | bytes 524288 | tf_op jit(solution)/shard_map/psum | solution.py:49
  37.9 22.8 %copy-start.2 = (bf16[128,2048]{1,0:T(8,128)(2,1)S(1)}, bf16[128,2048]{1,0:T(8,128)(2,1)}, u32[]{:S(2)}) copy-start(bf16[128,2048]{1,0:T(8,128)(2,1)} %param.15) | copy-start | bytes 1572868
  37.9 23.8 %copy-start.3 = (bf16[2048]{0:T(1024)(128)(2,1)S(1)}, bf16[2048]{0:T(1024)(128)(2,1)}, u32[]{:S(2)}) copy-start(bf16[2048]{0:T(1024)(128)(2,1)} %param.16) | copy-start | bytes 12292
  37.9 92.0 %copy-start.1 = (bf16[64,2048]{1,0:T(8,128)(2,1)S(1)}, bf16[64,2048]{1,0:T(8,128)(2,1)}, u32[]{:S(2)}) copy-start(bf16[64,2048]{1,0:T(8,128)(2,1)} %param.10) | copy-start | bytes 786436
  61.6 138.8 %all-reduce.5.cloned.1.call-start = ((), (), s32[]{:S(2)}) async-start(), calls=%async_computation.1 | async-start | bytes 524288 | tf_op jit(solution)/shard_map/psum | solution.py:49
Sparse Core Ops, SparseCore 0:
  61.7 68.1 all-reduce.2
  136.6 63.7 all-reduce.4
where the time goes:
time: 209 us
  waiting for transfers between devices  132 us (63%)
  matrix products  55.8 us (27%)
  between operations  13.5 us (6%)
  other arithmetic  7.41 us (4%)
    psum x2, waiting for transfers between devices, added(): lax.psum(term.astype(jnp.bfloat16), 'tp').astype(jnp.float32)  132 us
    dot_general x2, matrix products, einsum(): return jnp.einsum(form, a.astype(jnp.float32), b.astype(jnp.float32))  48.1 us
  transfers between devices with their start and end apart: 2, of which 2 were waited for; matrix products, arithmetic and copies ran while one was open for 0% of the time, Pallas kernels for 0%

commit v1 on v0

v1 whole, which is shorter than its diff:
```python
import functools

import jax
import jax.numpy as jnp
import numpy as np
from jax import lax
from jax.experimental import pallas as pl
from jax.experimental.pallas import tpu as pltpu
from jax.sharding import PartitionSpec as P

HEAD = 128
THETA = 10000
EPS = 1e-6
N = 16
BATCH = 64
CACHE = 4096
D = 2048
FF = 512
GROUP = 8
PAIRS = GROUP // 2
GROUPS = BATCH // GROUP
TILE = 256
TILES = CACHE // TILE
AHEAD = 8
SLOTS = 8
F32, BF16 = jnp.float32, jnp.bfloat16


def other(me, k):
    bits = [((me // 2**i) % 2 + (k >> i & 1)) % 2 * 2**i for i in range(4)]
    return bits[0] + bits[1] + bits[2] + bits[3]


ORDER = sorted(range(1, N), key=lambda k: -(bin(k >> 1).count("1") * 2 + (k & 1)))


def kernel(x_hbm, k_hbm, v_hbm, ga_hbm, wq_hbm, wo_hbm, gm_hbm, wg_hbm, wu_hbm, wd_hbm, rot_hbm, o_ref,
           x_v, ga_v, gm_v, wq_v, wo_v, wg_v, wu_v, wd_v, rot_v, a_v, q_v, s_v, p_v, seen_v, kbuf, vbuf,
           send_a, recv_a, h_all, send_m, recv_m, wsem, ksem, vsem, send_sem, recv_sem):
    me = lax.axis_index("tp")

    small = [pltpu.make_async_copy(src, dst, wsem.at[i]) for i, (src, dst) in enumerate((
        (x_hbm, x_v), (ga_hbm, ga_v), (wq_hbm, wq_v), (rot_hbm, rot_v)))]
    later = [pltpu.make_async_copy(src, dst, wsem.at[4 + i]) for i, (src, dst) in enumerate((
        (wo_hbm, wo_v), (gm_hbm, gm_v), (wg_hbm, wg_v), (wu_hbm, wu_v), (wd_hbm, wd_v)))]

    def pair_copy(hbm, buf, sem, pair):
        slot = lax.rem(pair, SLOTS)
        return pltpu.make_async_copy(hbm.at[pl.ds(pair * 2, 2)], buf.at[slot], sem.at[slot])

    def start_unit(u):
        group, phase, p = u // (2 * PAIRS), lax.rem(u // PAIRS, 2), lax.rem(u, PAIRS)
        pair = group * PAIRS + p

        @pl.when(jnp.logical_and(phase == 0, group < GROUPS))
        def _():
            pair_copy(k_hbm, kbuf, ksem, pair).start()

        @pl.when(jnp.logical_and(phase == 1, group < GROUPS))
        def _():
            pair_copy(v_hbm, vbuf, vsem, pair).start()

    for copy in small:
        copy.start()
    lax.fori_loop(0, AHEAD, lambda u, _: (start_unit(u), 0)[1], 0)

    barrier = pltpu.get_barrier_semaphore()
    for k in range(1, N):
        pl.semaphore_signal(barrier, inc=1, device_id={"tp": other(me, k)}, device_id_type=pl.DeviceIdType.MESH)

    def norm_into(columns, gain_v):
        total = jnp.zeros((BATCH, HEAD), F32)
        for c in range(N):
            wide = columns(c).astype(F32)
            total += wide * wide
        scale = lax.rsqrt(jnp.sum(total, -1, keepdims=True) / D + EPS)
        gain = gain_v[...].astype(F32)
        for c in range(N):
            a_v[:, c * HEAD:(c + 1) * HEAD] = (columns(c).astype(F32) * scale * gain[c:c + 1, :]).astype(BF16)

    for copy in small:
        copy.wait()
    norm_into(lambda c: x_v[:, c * HEAD:(c + 1) * HEAD], ga_v)
    q = jnp.dot(a_v[...], wq_v[...], preferred_element_type=F32).astype(BF16).astype(F32)
    q = q * rot_v[0:1, :] + pltpu.roll(q, HEAD // 2, 1) * rot_v[1:2, :]
    q_v[...] = q.astype(BF16).astype(F32)

    for copy in later:
        copy.start()

    rows = lax.broadcasted_iota(jnp.int32, (GROUP, HEAD), 0)

    def group_step(g, _):
        query = q_v[pl.ds(pl.multiple_of(g * GROUP, GROUP), GROUP), :]
        s_v[...] = jnp.zeros_like(s_v)

        def score_pair(p, _):
            pair = g * PAIRS + p
            slot = lax.rem(pair, SLOTS)
            pair_copy(k_hbm, kbuf, ksem, pair).wait()
            lhs = jnp.concatenate([jnp.where(rows == 2 * p, query, 0.0), jnp.where(rows == 2 * p + 1, query, 0.0)], 1).astype(BF16)
            for j in range(TILES):
                keys = slice(j * TILE, (j + 1) * TILE)
                rhs = jnp.concatenate([kbuf[slot, 0, keys, :], kbuf[slot, 1, keys, :]], 1)
                s_v[:, keys] += lax.dot_general(lhs, rhs, (((1,), (1,)), ((), ())), preferred_element_type=F32)
            start_unit(g * 2 * PAIRS + p + AHEAD)
            return 0

        lax.fori_loop(0, PAIRS, score_pair, 0)

        scores = s_v[...] * HEAD**-0.5
        e = jnp.exp(scores - jnp.max(scores, -1, keepdims=True))
        p_v[...] = (e * (1.0 / jnp.sum(e, -1, keepdims=True))).astype(BF16)

        def value_pair(p, seen):
            pair = g * PAIRS + p
            slot = lax.rem(pair, SLOTS)
            pair_copy(v_hbm, vbuf, vsem, pair).wait()
            acc = [jnp.zeros((GROUP, 2 * HEAD), F32) for _ in range(2)]
            for j in range(TILES):
                keys = slice(j * TILE, (j + 1) * TILE)
                rhs = jnp.concatenate([vbuf[slot, 0, keys, :], vbuf[slot, 1, keys, :]], 1)
                acc[j % 2] += jnp.dot(p_v[:, keys], rhs, preferred_element_type=F32)
            out = acc[0] + acc[1]
            start_unit(g * 2 * PAIRS + PAIRS + p + AHEAD)
            return jnp.where(rows == 2 * p, out[:, :HEAD], jnp.where(rows == 2 * p + 1, out[:, HEAD:], seen))

        seen = lax.fori_loop(0, PAIRS, value_pair, jnp.zeros((GROUP, HEAD), F32))
        seen_v[pl.ds(pl.multiple_of(g * GROUP, GROUP), GROUP), :] = seen
        return 0

    lax.fori_loop(0, GROUPS, group_step, 0)

    for copy in later:
        copy.wait()
    pl.semaphore_wait(barrier, N - 1)

    mine = pl.ds(pl.multiple_of(me * HEAD, HEAD), HEAD)

    def exchange(phase, source, target):
        copies = {}
        for k in ORDER:
            peer = other(me, k)
            copies[k] = pltpu.make_async_remote_copy(
                src_ref=source(peer), dst_ref=target(k), send_sem=send_sem.at[phase, k], recv_sem=recv_sem.at[phase, k],
                device_id={"tp": peer}, device_id_type=pl.DeviceIdType.MESH)
            copies[k].start()
        return copies

    def summed(phase, left, w_v, send, recv, base):
        for c in range(0, N, 2):
            term = jnp.dot(left, w_v[:, c * HEAD:(c + 2) * HEAD], preferred_element_type=F32).astype(BF16)
            send[c] = term[:, :HEAD]
            send[c + 1] = term[:, HEAD:]
        copies = exchange(phase, lambda peer: send.at[peer], lambda k: recv.at[k])
        total = base + jnp.dot(left, w_v[:, mine], preferred_element_type=F32)
        for k in reversed(ORDER):
            copies[k].wait_recv()
            total += recv[k].astype(F32)
        return total, copies

    h, sent = summed(0, seen_v[...].astype(BF16), wo_v, send_a, recv_a, x_v[:, mine].astype(F32))
    h_all[me] = h.astype(BF16)
    spread = exchange(1, lambda peer: h_all.at[me], lambda k: h_all.at[me])

    def arrived(phase, k, ref):
        peer = other(me, k)
        pltpu.make_async_remote_copy(
            src_ref=ref(me), dst_ref=ref(peer), send_sem=send_sem.at[phase, k], recv_sem=recv_sem.at[phase, k],
            device_id={"tp": peer}, device_id_type=pl.DeviceIdType.MESH).wait_recv()

    for k in reversed(ORDER):
        arrived(1, k, lambda c: h_all.at[c])
    norm_into(lambda c: h_all[c], gm_v)
    gate = jnp.dot(a_v[...], wg_v[...], preferred_element_type=F32)
    up = jnp.dot(a_v[...], wu_v[...], preferred_element_type=F32)
    hidden = (gate * (1.0 / (1.0 + jnp.exp(-gate))) * up).astype(BF16)
    y, sent_m = summed(2, hidden, wd_v, send_m, recv_m, h_all[me].astype(F32))
    o_ref[:, mine] = y.astype(BF16)
    spread_m = exchange(3, lambda peer: o_ref.at[:, mine], lambda k: o_ref.at[:, mine])
    for k in reversed(ORDER):
        arrived(3, k, lambda c: o_ref.at[:, pl.ds(pl.multiple_of(c * HEAD, HEAD), HEAD)])
    for copies in (sent, spread, sent_m, spread_m):
        for k in ORDER:
            copies[k].wait_send()


def rotary_table():
    half = HEAD // 2
    angle = (CACHE - 1) * THETA ** (-np.arange(half, dtype=np.float64) / half)
    cos, sin = np.cos(angle), np.sin(angle)
    table = np.zeros((8, HEAD), np.float32)
    table[0], table[1] = np.concatenate([cos, cos]), np.concatenate([-sin, sin])
    return table


def solution(mesh):
    def step(x, k_cache, v_cache, gain_a, wq, wo, gain_m, w_gate, w_up, w_down):
        whole = pl.BlockSpec(memory_space=pl.ANY)
        call = pl.pallas_call(
            kernel,
            out_shape=jax.ShapeDtypeStruct((BATCH, D), BF16),
            in_specs=[whole] * 11,
            out_specs=pl.BlockSpec(memory_space=pltpu.VMEM),
            scratch_shapes=[
                pltpu.VMEM((BATCH, D), BF16), pltpu.VMEM((N, HEAD), BF16), pltpu.VMEM((N, HEAD), BF16),
                pltpu.VMEM((D, HEAD), BF16), pltpu.VMEM((HEAD, D), BF16), pltpu.VMEM((D, FF), BF16), pltpu.VMEM((D, FF), BF16),
                pltpu.VMEM((FF, D), BF16), pltpu.VMEM((8, HEAD), F32), pltpu.VMEM((BATCH, D), BF16), pltpu.VMEM((BATCH, HEAD), F32),
                pltpu.VMEM((GROUP, CACHE), F32), pltpu.VMEM((GROUP, CACHE), BF16), pltpu.VMEM((BATCH, HEAD), F32),
                pltpu.VMEM((SLOTS, 2, CACHE, HEAD), BF16), pltpu.VMEM((SLOTS, 2, CACHE, HEAD), BF16),
                pltpu.VMEM((N, BATCH, HEAD), BF16), pltpu.VMEM((N, BATCH, HEAD), BF16), pltpu.VMEM((N, BATCH, HEAD), BF16),
                pltpu.VMEM((N, BATCH, HEAD), BF16), pltpu.VMEM((N, BATCH, HEAD), BF16),
                pltpu.SemaphoreType.DMA((9,)), pltpu.SemaphoreType.DMA((SLOTS,)), pltpu.SemaphoreType.DMA((SLOTS,)),
                pltpu.SemaphoreType.DMA((4, N)), pltpu.SemaphoreType.DMA((4, N)),
            ],
            compiler_params=pltpu.CompilerParams(collective_id=0, has_side_effects=True, vmem_limit_bytes=60 * 2**20),
            name="decode_layer",
        )
        return call(x, k_cache.reshape(BATCH, CACHE, HEAD), v_cache.reshape(BATCH, CACHE, HEAD), gain_a.reshape(N, HEAD), wq, wo,
                    gain_m.reshape(N, HEAD), w_gate, w_up, w_down, jnp.asarray(rotary_table()))

    states, cache, columns, rows_of = P("dp", None), P("dp", None, "tp", None), P(None, "tp"), P("tp", None)
    return jax.shard_map(
        step,
        mesh=mesh,
        in_specs=(states, cache, cache, P(None), columns, rows_of, P(None), columns, columns, rows_of),
        out_specs=states,
        check_vma=False,
    )
```

time: 209 us -> 70.3 us (0.34)
  waiting for transfers between devices: 132 us -> 0 us
  Pallas kernels: 0 us -> 68.5 us
  matrix products: 55.8 us -> 0 us
  between operations: 13.5 us -> 0.01 us
  other arithmetic: 7.41 us -> 0 us
    psum x2 -> x0, waiting for transfers between devices: 132 us -> none  [added(): lax.psum(term.astype(jnp.bfloat16), 'tp').astype(jnp.float32)]
    pallas_call x0 -> x1, Pallas kernels: none -> 68.5 us  [step(): call(x, k_cache.reshape(BATCH, CACHE, HEAD), v_cache.reshape(BATCH, CACHE...]
    dot_general x6 -> x0, matrix products: 55.8 us -> none  [the longest x2 48.1 us: einsum(): return jnp.einsum(form, a.astype(jnp.float32), b.astype(jnp.float32))]
    convert_element_type x4 -> x0, other arithmetic: 3.38 us -> none  [the longest x1 1.71 us: added(): (t.astype(jnp.float32) + lax.psum(term.astype(jnp.bfloat16), 'tp').astype...]
    reduce_sum x3 -> x0, other arithmetic: 3.03 us -> none  [the longest x2 2.24 us: normed(): scale = lax.rsqrt(jnp.mean(wide * wide, -1, keepdims=True) + 1e-06)]
  transfers between devices with their start and end apart: 2 -> 0, of which waited for: 2 -> 0; matrix products, arithmetic and copies ran while one was open for 0% -> 0% of each run, Pallas kernels for 0% -> 0%
where the time goes in v1:
time: 70.3 us; the launch traced here: 70.2 us
  Pallas kernels  68.5 us (97%)
  local copies, waits for them, and re-layouts  1.67 us (2%)
    pallas_call x1, Pallas kernels, step(): call(x, k_cache.reshape(BATCH, CACHE, HEAD), v_cache.reshape(BATCH, CACHE...  68.5 us
    unnamed x1, local copies, waits for them, and re-layouts  1.67 us

profile of v1, /device:TPU:0, one launch (start us, length us, event | category | flops | bytes accessed | tf_op | source)
XLA Modules:
  0.0 70.2 jit_solution(14526372574730797344)
XLA Ops:
  0.0 68.5 %decode_layer.1 = bf16[64,2048]{1,0:T(8,128)(2,1)} custom-call(bf16[64,2048]{1,0:T(8,128)(2,1)} %x_hbm.1, bf16[64,4096,128]{2,1,0:T(8,128)(2,1)} %bitcast.k_hbm, bf16[64,4096,128]{2,1,0:T(8,128)(2,1)} %bitcast.1.v_hbm, bf16[16,128]{1,0:T(8,128)(2,1)} %bitcast.4, bf16[2048,128]{1,0:T(8,128)(2,1)} %wq_hbm.1, bf16[128,2048]{1,0:T(8,128)(2,1)} %wo_hbm.1, ...), custom_call_target="tpu_custom_call" | custom-call | tf_op jit(solution)/shard_map/decode_layer/pallas_call | solution.py:219
  68.5 1.7 %copy.13 = bf16[64,2048]{1,0:T(8,128)(2,1)} copy(bf16[64,2048]{1,0:T(8,128)(2,1)} %decode_layer.1) | data formatting | bytes 524288

commit v2 on v0

v2 whole, which is shorter than its diff:
```python
import functools

import jax
import jax.numpy as jnp
import numpy as np
from jax import lax
from jax.experimental import pallas as pl
from jax.experimental.pallas import tpu as pltpu
from jax.sharding import PartitionSpec as P

HEAD = 128
THETA = 10000
EPS = 1e-6
N = 16
BATCH = 64
CACHE = 4096
D = 2048
FF = 512
GROUP = 4
ROWS = 8
GROUPS = BATCH // GROUP
TILE = 256
TILES = CACHE // TILE
SLOTS = 3
WIDE = D // 2
F32, BF16 = jnp.float32, jnp.bfloat16

PARTS = ((0, 32, 32), (32, 32, 24))
LAST = (14, 15)
PHASES = 4 * len(PARTS) + len(LAST)


def other(me, k):
    bits = [((me // 2**i) % 2 + (k >> i & 1)) % 2 * 2**i for i in range(4)]
    return bits[0] + bits[1] + bits[2] + bits[3]


ORDER = sorted(range(1, N), key=lambda k: -(bin(k >> 1).count("1") * 2 + (k & 1)))


def kernel(x_hbm, k_hbm, v_hbm, ga_hbm, wq_hbm, wo_hbm, gm_hbm, wg_hbm, wu_hbm, wd_hbm, rot_hbm, o_ref,
           x_v, ga_v, gm_v, wq_v, wo_v, wg_v, wu_v, wd_v, rot_v, a_v, q_v, s_v, p_v, seen_v, kbuf, vbuf,
           part_bufs, last_bufs, wsem, ksem, vsem, send_sem, recv_sem):
    me = lax.axis_index("tp")
    peers = {k: other(me, k) for k in range(1, N)}
    mine = pl.ds(pl.multiple_of(me * HEAD, HEAD), HEAD)

    small = [pltpu.make_async_copy(src, dst, wsem.at[i]) for i, (src, dst) in enumerate((
        (x_hbm, x_v), (ga_hbm, ga_v), (wq_hbm, wq_v), (rot_hbm, rot_v)))]
    middle = [pltpu.make_async_copy(src, dst, wsem.at[7 + i]) for i, (src, dst) in enumerate(((wo_hbm, wo_v), (gm_hbm, gm_v)))]
    later = [pltpu.make_async_copy(src, dst, wsem.at[4 + i]) for i, (src, dst) in enumerate((
        (wg_hbm, wg_v), (wu_hbm, wu_v), (wd_hbm, wd_v)))]

    def keys_copy(g):
        slot = lax.rem(g, SLOTS)
        return pltpu.make_async_copy(k_hbm.at[pl.ds(g * GROUP, GROUP)], kbuf.at[slot], ksem.at[slot])

    def values_copy(g):
        slot = lax.rem(g, SLOTS)
        return pltpu.make_async_copy(v_hbm.at[pl.ds(g * GROUP, GROUP)], vbuf.at[slot], vsem.at[slot])

    for copy in small:
        copy.start()
    keys_copy(0).start()
    keys_copy(1).start()
    values_copy(0).start()
    keys_copy(2).start()
    values_copy(1).start()

    barrier = pltpu.get_barrier_semaphore()
    for k in range(1, N):
        pl.semaphore_signal(barrier, inc=1, device_id={"tp": peers[k]}, device_id_type=pl.DeviceIdType.MESH)

    def norm_into(first, rows, columns, gain_v):
        total = jnp.zeros((rows, HEAD), F32)
        for c in range(N):
            wide = columns(c).astype(F32)
            total += wide * wide
        scale = lax.rsqrt(jnp.sum(total, -1, keepdims=True) / D + EPS)
        gain = gain_v[...].astype(F32)
        for c in range(N):
            a_v[first:first + rows, c * HEAD:(c + 1) * HEAD] = (columns(c).astype(F32) * scale * gain[c:c + 1, :]).astype(BF16)

    for copy in small:
        copy.wait()
    norm_into(0, BATCH, lambda c: x_v[:, c * HEAD:(c + 1) * HEAD], ga_v)
    q = jnp.dot(a_v[...], wq_v[...], preferred_element_type=F32).astype(BF16).astype(F32)
    q = q * rot_v[0:1, :] + pltpu.roll(q, HEAD // 2, 1) * rot_v[1:2, :]
    q = q.astype(BF16).astype(F32)
    for g in range(GROUPS):
        q_v[g, :GROUP] = q[g * GROUP:(g + 1) * GROUP]

    for copy in middle:
        copy.start()

    rows = lax.broadcasted_iota(jnp.int32, (ROWS, HEAD), 0)

    def score(g):
        slot = lax.rem(g, SLOTS)
        query = q_v[g]
        own = [jnp.where(rows == i, query, 0.0) for i in range(GROUP)]
        lhs = [jnp.concatenate(own[i:i + 2], 1).astype(BF16) for i in range(0, GROUP, 2)]
        for j in range(TILES):
            keys = slice(j * TILE, (j + 1) * TILE)
            total = None
            for i in range(0, GROUP, 2):
                rhs = jnp.concatenate([kbuf[slot, i, keys, :], kbuf[slot, i + 1, keys, :]], 1)
                part = lax.dot_general(lhs[i // 2], rhs, (((1,), (1,)), ((), ())), preferred_element_type=F32)
                total = part if total is None else total + part
            s_v[:, keys] = total

    def weigh(g):
        scores = s_v[...] * HEAD**-0.5
        e = jnp.exp(scores - jnp.max(scores, -1, keepdims=True))
        p_v[lax.rem(g, 2)] = (e * (1.0 / jnp.sum(e, -1, keepdims=True))).astype(BF16)

    def gather(g):
        slot, place = lax.rem(g, SLOTS), lax.rem(g, 2)
        seen = jnp.zeros((ROWS, HEAD), F32)
        for i in range(0, GROUP, 2):
            out = None
            for j in range(TILES):
                keys = slice(j * TILE, (j + 1) * TILE)
                rhs = jnp.concatenate([vbuf[slot, i, keys, :], vbuf[slot, i + 1, keys, :]], 1)
                part = jnp.dot(p_v[place, :, keys], rhs, preferred_element_type=F32)
                out = part if out is None else out + part
            seen = jnp.where(rows == i, out[:, :HEAD], jnp.where(rows == i + 1, out[:, HEAD:], seen))
        seen_v[g] = seen

    def copy(phase, k, source, target):
        return pltpu.make_async_remote_copy(
            src_ref=source, dst_ref=target, send_sem=send_sem.at[phase], recv_sem=recv_sem.at[phase],
            device_id={"tp": peers[k]}, device_id_type=pl.DeviceIdType.MESH)

    def start(phase, source, target):
        for k in ORDER:
            copy(phase, k, source(k), target(k)).start()

    def arrived(phase, size):
        copy(phase, 1, size, size).wait_recv()

    def left_here(phase, size):
        copy(phase, 1, size, size).wait_send()

    def block_of(i, owner):
        first, count, _ = PARTS[i]
        return o_ref.at[first:first + count, pl.ds(pl.multiple_of(owner * HEAD, HEAD), HEAD)]

    def size_of(i, phase):
        first, count, _ = PARTS[i]
        return o_ref.at[first:first + count, :(N - 1) * HEAD] if phase == 3 else part_bufs[i][phase].at[:N - 1]

    def left_of(i, phase):
        first, _, direct = PARTS[i]
        if phase == 0:
            return jnp.concatenate([seen_v[g, :GROUP] for g in range(first // GROUP, (first + direct) // GROUP)], 0).astype(BF16)
        return part_bufs[i][5][...]

    def send_terms(i, phase, w_v):
        left, send = left_of(i, phase), part_bufs[i][phase]
        for c in range(0, N, 2):
            term = jnp.dot(left, w_v[:, c * HEAD:(c + 2) * HEAD], preferred_element_type=F32).astype(BF16)
            send[c] = term[:, :HEAD]
            send[c + 1] = term[:, HEAD:]
        recv = part_bufs[i][phase + 1]
        start(4 * i + phase, lambda k: send.at[peers[k]], lambda k: recv.at[k])

    def finished(i, phase, w_v, base):
        recv = part_bufs[i][phase + 1]
        total = base + jnp.dot(left_of(i, phase), w_v[:, mine], preferred_element_type=F32)
        arrived(4 * i + phase, size_of(i, phase))
        for k in range(1, N):
            total += recv[k].astype(F32)
        return total.astype(BF16)

    def part_a(i):
        send_terms(i, 0, wo_v)

    def part_b(i):
        first, _, direct = PARTS[i]
        part_bufs[i][4][me, :direct] = finished(i, 0, wo_v, x_v[first:first + direct, mine].astype(F32))
        block = part_bufs[i][4].at[me, :PARTS[i][2]]
        start(4 * i + 1, lambda k: block, lambda k: block)

    def part_c(i):
        first, count, direct = PARTS[i]
        h_all, hidden_v = part_bufs[i][4:]
        arrived(4 * i + 1, size_of(i, 1))
        for j, at in enumerate(range(first + direct, first + count, ROWS)):
            h = unpacked(*(first_sum(2 * j + r) for r in range(2)))
            for c in range(N):
                h_all[c, direct + j * ROWS:direct + (j + 1) * ROWS] = h[c // (N // 2)][:, c % (N // 2) * HEAD:(c % (N // 2) + 1) * HEAD].astype(BF16)
        norm_into(first, count, lambda c: h_all[c], gm_v)
        a = a_v[first:first + count]
        gate = jnp.dot(a, wg_v[...], preferred_element_type=F32)
        up = jnp.dot(a, wu_v[...], preferred_element_type=F32)
        hidden_v[...] = (gate * (1.0 / (1.0 + jnp.exp(-gate))) * up).astype(BF16)
        send_terms(i, 2, wd_v)

    def part_d(i):
        block_of(i, me)[...] = finished(i, 2, wd_v, part_bufs[i][4][me].astype(F32))
        start(4 * i + 3, lambda k: block_of(i, me), lambda k: block_of(i, me))

    def part_e(i):
        arrived(4 * i + 3, size_of(i, 3))

    low = lax.broadcasted_iota(jnp.int32, (ROWS, 1), 0) < GROUP

    def packed(left, right):
        return jnp.where(low, left, right)

    def swap(t):
        return pltpu.roll(t, GROUP, 0)

    def last_phase(i):
        return 4 * len(PARTS) + i

    def send_whole(i, left, w_v):
        recv = last_bufs[i]
        for c in range(0, WIDE, 2 * HEAD):
            term = [jnp.dot(left, w_v[:, at:at + 2 * HEAD], preferred_element_type=F32) for at in (c, WIDE + c)]
            recv[me, :, c:c + 2 * HEAD] = packed(*term).astype(BF16)
        start(last_phase(i), lambda k: recv.at[me], lambda k: recv.at[me])

    def added(i, base):
        recv = last_bufs[i]
        arrived(last_phase(i), recv.at[:N - 1])
        total = recv[0].astype(F32)
        for d in range(1, N):
            total += recv[d].astype(F32)
        return (base + total).astype(BF16).astype(F32)

    def last_a(i):
        seen = seen_v[LAST[i]].astype(BF16).astype(F32)
        send_whole(i, (seen + swap(seen)).astype(BF16), wo_v)

    def unpacked(a, b):
        return packed(a, swap(b)), packed(swap(a), b)

    def first_sum(i):
        first = LAST[i] * GROUP // ROWS * ROWS
        x = x_v[first:first + ROWS, :].astype(F32)
        left, right = x[:, :WIDE], x[:, WIDE:]
        return added(i, packed(left, swap(right)) if LAST[i] * GROUP == first else packed(swap(left), right))

    keys_copy(0).wait()
    score(0)
    weigh(0)

    def entered():
        for c in middle:
            c.wait()
        pl.semaphore_wait(barrier, N - 1)

    stages = {
        6: (entered,), 7: (lambda: part_a(0),), 9: (lambda: part_b(0),), 13: (lambda: part_a(1),), 14: (lambda: last_a(0),)}

    def step(g, _):
        keys_copy(g + 1).wait()
        values_copy(g).wait()

        @pl.when(g + 3 < GROUPS)
        def _():
            keys_copy(g + 3).start()

        @pl.when(g + 2 < GROUPS)
        def _():
            values_copy(g + 2).start()

        @pl.when(g + 3 == GROUPS)
        def _():
            for c in later:
                c.start()

        score(g + 1)
        gather(g)
        weigh(g + 1)

        for when, jobs in stages.items():
            @pl.when(g == when)
            def _():
                for job in jobs:
                    job()

        return 0

    lax.fori_loop(0, GROUPS - 1, step, 0)
    values_copy(GROUPS - 1).wait()
    gather(GROUPS - 1)
    last_a(1)
    part_b(1)
    for c in later:
        c.wait()
    part_c(0)
    part_c(1)
    part_d(0)
    part_d(1)
    part_e(0)
    part_e(1)
    for i in range(len(PARTS)):
        for phase in range(4):
            left_here(4 * i + phase, size_of(i, phase))
    for i in range(len(LAST)):
        left_here(last_phase(i), last_bufs[i].at[:N - 1])


def rotary_table():
    half = HEAD // 2
    angle = (CACHE - 1) * THETA ** (-np.arange(half, dtype=np.float64) / half)
    cos, sin = np.cos(angle), np.sin(angle)
    table = np.zeros((8, HEAD), np.float32)
    table[0], table[1] = np.concatenate([cos, cos]), np.concatenate([-sin, sin])
    return table


def solution(mesh):
    def step(x, k_cache, v_cache, gain_a, wq, wo, gain_m, w_gate, w_up, w_down):
        whole = pl.BlockSpec(memory_space=pl.ANY)
        call = pl.pallas_call(
            kernel,
            out_shape=jax.ShapeDtypeStruct((BATCH, D), BF16),
            in_specs=[whole] * 11,
            out_specs=pl.BlockSpec(memory_space=pltpu.VMEM),
            scratch_shapes=[
                pltpu.VMEM((BATCH, D), BF16), pltpu.VMEM((N, HEAD), BF16), pltpu.VMEM((N, HEAD), BF16),
                pltpu.VMEM((D, HEAD), BF16), pltpu.VMEM((HEAD, D), BF16), pltpu.VMEM((D, FF), BF16), pltpu.VMEM((D, FF), BF16),
                pltpu.VMEM((FF, D), BF16), pltpu.VMEM((8, HEAD), F32), pltpu.VMEM((BATCH, D), BF16), pltpu.VMEM((GROUPS, ROWS, HEAD), F32),
                pltpu.VMEM((ROWS, CACHE), F32), pltpu.VMEM((2, ROWS, CACHE), BF16), pltpu.VMEM((GROUPS, ROWS, HEAD), F32),
                pltpu.VMEM((SLOTS, GROUP, CACHE, HEAD), BF16), pltpu.VMEM((SLOTS, GROUP, CACHE, HEAD), BF16),
                [[pltpu.VMEM((N, rows, HEAD), BF16) for rows in (direct, direct, count, count, count)] + [pltpu.VMEM((count, FF), BF16)]
                 for _, count, direct in PARTS],
                [pltpu.VMEM((N, ROWS, WIDE), BF16) for _ in LAST],
                pltpu.SemaphoreType.DMA((9,)), pltpu.SemaphoreType.DMA((SLOTS,)), pltpu.SemaphoreType.DMA((SLOTS,)),
                pltpu.SemaphoreType.DMA((PHASES,)), pltpu.SemaphoreType.DMA((PHASES,)),
            ],
            compiler_params=pltpu.CompilerParams(collective_id=0, has_side_effects=True, vmem_limit_bytes=60 * 2**20),
            name="decode_layer",
        )
        return call(x, k_cache.reshape(BATCH, CACHE, HEAD), v_cache.reshape(BATCH, CACHE, HEAD), gain_a.reshape(N, HEAD), wq, wo,
                    gain_m.reshape(N, HEAD), w_gate, w_up, w_down, jnp.asarray(rotary_table()))

    states, cache, columns, rows_of = P("dp", None), P("dp", None, "tp", None), P(None, "tp"), P("tp", None)
    return jax.shard_map(
        step,
        mesh=mesh,
        in_specs=(states, cache, cache, P(None), columns, rows_of, P(None), columns, columns, rows_of),
        out_specs=states,
        check_vma=False,
    )
```

time: 209 us -> 67 us (0.32)
  waiting for transfers between devices: 132 us -> 0 us
  Pallas kernels: 0 us -> 65.2 us
  matrix products: 55.8 us -> 0 us
  between operations: 13.5 us -> 0.01 us
  other arithmetic: 7.41 us -> 0 us
    psum x2 -> x0, waiting for transfers between devices: 132 us -> none  [added(): lax.psum(term.astype(jnp.bfloat16), 'tp').astype(jnp.float32)]
    pallas_call x0 -> x1, Pallas kernels: none -> 65.2 us  [step(): call(x, k_cache.reshape(BATCH, CACHE, HEAD), v_cache.reshape(BATCH, CACHE...]
    dot_general x6 -> x0, matrix products: 55.8 us -> none  [the longest x2 48.1 us: einsum(): return jnp.einsum(form, a.astype(jnp.float32), b.astype(jnp.float32))]
    convert_element_type x4 -> x0, other arithmetic: 3.38 us -> none  [the longest x1 1.71 us: added(): (t.astype(jnp.float32) + lax.psum(term.astype(jnp.bfloat16), 'tp').astype...]
    reduce_sum x3 -> x0, other arithmetic: 3.03 us -> none  [the longest x2 2.24 us: normed(): scale = lax.rsqrt(jnp.mean(wide * wide, -1, keepdims=True) + 1e-06)]
  transfers between devices with their start and end apart: 2 -> 0, of which waited for: 2 -> 0; matrix products, arithmetic and copies ran while one was open for 0% -> 0% of each run, Pallas kernels for 0% -> 0%
where the time goes in v2:
time: 67 us; the launch traced here: 66.9 us
  Pallas kernels  65.2 us (97%)
  local copies, waits for them, and re-layouts  1.67 us (2%)
    pallas_call x1, Pallas kernels, step(): call(x, k_cache.reshape(BATCH, CACHE, HEAD), v_cache.reshape(BATCH, CACHE...  65.2 us
    unnamed x1, local copies, waits for them, and re-layouts  1.67 us

profile of v2, /device:TPU:0, one launch (start us, length us, event | category | flops | bytes accessed | tf_op | source)
XLA Modules:
  0.0 66.9 jit_solution(16699562041538195494)
XLA Ops:
  0.0 65.2 %decode_layer.1 = bf16[64,2048]{1,0:T(8,128)(2,1)} custom-call(bf16[64,2048]{1,0:T(8,128)(2,1)} %x_hbm.1, bf16[64,4096,128]{2,1,0:T(8,128)(2,1)} %bitcast.k_hbm, bf16[64,4096,128]{2,1,0:T(8,128)(2,1)} %bitcast.1.v_hbm, bf16[16,128]{1,0:T(8,128)(2,1)} %bitcast.4, bf16[2048,128]{1,0:T(8,128)(2,1)} %wq_hbm.1, bf16[128,2048]{1,0:T(8,128)(2,1)} %wo_hbm.1, ...), custom_call_target="tpu_custom_call" | custom-call | tf_op jit(solution)/shard_map/decode_layer/pallas_call | solution.py:339
  65.2 1.7 %copy.13 = bf16[64,2048]{1,0:T(8,128)(2,1)} copy(bf16[64,2048]{1,0:T(8,128)(2,1)} %decode_layer.1) | data formatting | bytes 524288

commit v3 on v2

--- a/solution.py
+++ b/solution.py
@@ -21,13 +21,17 @@
 GROUPS = BATCH // GROUP
 TILE = 256
 TILES = CACHE // TILE
+WEIGHTS_AT = 7
 SLOTS = 3
-WIDE = D // 2
 F32, BF16 = jnp.float32, jnp.bfloat16
 
-PARTS = ((0, 32, 32), (32, 32, 24))
-LAST = (14, 15)
-PHASES = 4 * len(PARTS) + len(LAST)
+PARTS = ((0, 32), (32, 24))
+EARLY = sum(rows for _, rows in PARTS)
+LATE = BATCH - EARLY
+LATE_AT = 4 * len(PARTS)
+OWNERS = ((15, 7, 11, 13), (1, 3, 5, 9))
+PART = D // len(OWNERS[0])
+PHASES = LATE_AT + 4
 
 
 def other(me, k):
@@ -40,7 +44,7 @@
 
 def kernel(x_hbm, k_hbm, v_hbm, ga_hbm, wq_hbm, wo_hbm, gm_hbm, wg_hbm, wu_hbm, wd_hbm, rot_hbm, o_ref,
            x_v, ga_v, gm_v, wq_v, wo_v, wg_v, wu_v, wd_v, rot_v, a_v, q_v, s_v, p_v, seen_v, kbuf, vbuf,
-           part_bufs, last_bufs, wsem, ksem, vsem, send_sem, recv_sem):
+           part_bufs, late_bufs, wsem, ksem, vsem, send_sem, recv_sem):
     me = lax.axis_index("tp")
     peers = {k: other(me, k) for k in range(1, N)}
     mine = pl.ds(pl.multiple_of(me * HEAD, HEAD), HEAD)
@@ -142,106 +146,116 @@
     def left_here(phase, size):
         copy(phase, 1, size, size).wait_send()
 
-    def block_of(i, owner):
-        first, count, _ = PARTS[i]
-        return o_ref.at[first:first + count, pl.ds(pl.multiple_of(owner * HEAD, HEAD), HEAD)]
-
-    def size_of(i, phase):
-        first, count, _ = PARTS[i]
-        return o_ref.at[first:first + count, :(N - 1) * HEAD] if phase == 3 else part_bufs[i][phase].at[:N - 1]
-
-    def left_of(i, phase):
-        first, _, direct = PARTS[i]
-        if phase == 0:
-            return jnp.concatenate([seen_v[g, :GROUP] for g in range(first // GROUP, (first + direct) // GROUP)], 0).astype(BF16)
-        return part_bufs[i][5][...]
-
-    def send_terms(i, phase, w_v):
-        left, send = left_of(i, phase), part_bufs[i][phase]
+    late_send, late_recv, late_send_m, late_recv_m, late_h, late_hidden = late_bufs
+
+    def seen_rows(first, count):
+        return jnp.concatenate([seen_v[g, :GROUP] for g in range(first // GROUP, (first + count) // GROUP)], 0).astype(BF16)
+
+    def hidden_rows(first, count, columns, hidden_v):
+        norm_into(first, count, columns, gm_v)
+        a = a_v[first:first + count]
+        gate = jnp.dot(a, wg_v[...], preferred_element_type=F32)
+        up = jnp.dot(a, wu_v[...], preferred_element_type=F32)
+        hidden_v[...] = (gate * (1.0 / (1.0 + jnp.exp(-gate))) * up).astype(BF16)
+
+    def early_terms(phase, left, w_v, send, recv):
         for c in range(0, N, 2):
             term = jnp.dot(left, w_v[:, c * HEAD:(c + 2) * HEAD], preferred_element_type=F32).astype(BF16)
             send[c] = term[:, :HEAD]
             send[c + 1] = term[:, HEAD:]
-        recv = part_bufs[i][phase + 1]
-        start(4 * i + phase, lambda k: send.at[peers[k]], lambda k: recv.at[k])
-
-    def finished(i, phase, w_v, base):
-        recv = part_bufs[i][phase + 1]
-        total = base + jnp.dot(left_of(i, phase), w_v[:, mine], preferred_element_type=F32)
-        arrived(4 * i + phase, size_of(i, phase))
+        start(phase, lambda k: send.at[peers[k]], lambda k: recv.at[k])
+
+    def early_sum(phase, left, w_v, recv, base):
+        total = base + jnp.dot(left, w_v[:, mine], preferred_element_type=F32)
+        arrived(phase, recv.at[:N - 1])
         for k in range(1, N):
             total += recv[k].astype(F32)
         return total.astype(BF16)
 
-    def part_a(i):
-        send_terms(i, 0, wo_v)
-
-    def part_b(i):
-        first, _, direct = PARTS[i]
-        part_bufs[i][4][me, :direct] = finished(i, 0, wo_v, x_v[first:first + direct, mine].astype(F32))
-        block = part_bufs[i][4].at[me, :PARTS[i][2]]
-        start(4 * i + 1, lambda k: block, lambda k: block)
-
-    def part_c(i):
-        first, count, direct = PARTS[i]
-        h_all, hidden_v = part_bufs[i][4:]
-        arrived(4 * i + 1, size_of(i, 1))
-        for j, at in enumerate(range(first + direct, first + count, ROWS)):
-            h = unpacked(*(first_sum(2 * j + r) for r in range(2)))
-            for c in range(N):
-                h_all[c, direct + j * ROWS:direct + (j + 1) * ROWS] = h[c // (N // 2)][:, c % (N // 2) * HEAD:(c % (N // 2) + 1) * HEAD].astype(BF16)
-        norm_into(first, count, lambda c: h_all[c], gm_v)
-        a = a_v[first:first + count]
-        gate = jnp.dot(a, wg_v[...], preferred_element_type=F32)
-        up = jnp.dot(a, wu_v[...], preferred_element_type=F32)
-        hidden_v[...] = (gate * (1.0 / (1.0 + jnp.exp(-gate))) * up).astype(BF16)
-        send_terms(i, 2, wd_v)
-
-    def part_d(i):
-        block_of(i, me)[...] = finished(i, 2, wd_v, part_bufs[i][4][me].astype(F32))
-        start(4 * i + 3, lambda k: block_of(i, me), lambda k: block_of(i, me))
-
-    def part_e(i):
-        arrived(4 * i + 3, size_of(i, 3))
-
-    low = lax.broadcasted_iota(jnp.int32, (ROWS, 1), 0) < GROUP
-
-    def packed(left, right):
-        return jnp.where(low, left, right)
-
-    def swap(t):
-        return pltpu.roll(t, GROUP, 0)
-
-    def last_phase(i):
-        return 4 * len(PARTS) + i
-
-    def send_whole(i, left, w_v):
-        recv = last_bufs[i]
-        for c in range(0, WIDE, 2 * HEAD):
-            term = [jnp.dot(left, w_v[:, at:at + 2 * HEAD], preferred_element_type=F32) for at in (c, WIDE + c)]
-            recv[me, :, c:c + 2 * HEAD] = packed(*term).astype(BF16)
-        start(last_phase(i), lambda k: recv.at[me], lambda k: recv.at[me])
-
-    def added(i, base):
-        recv = last_bufs[i]
-        arrived(last_phase(i), recv.at[:N - 1])
-        total = recv[0].astype(F32)
-        for d in range(1, N):
-            total += recv[d].astype(F32)
-        return (base + total).astype(BF16).astype(F32)
-
-    def last_a(i):
-        seen = seen_v[LAST[i]].astype(BF16).astype(F32)
-        send_whole(i, (seen + swap(seen)).astype(BF16), wo_v)
-
-    def unpacked(a, b):
-        return packed(a, swap(b)), packed(swap(a), b)
-
-    def first_sum(i):
-        first = LAST[i] * GROUP // ROWS * ROWS
-        x = x_v[first:first + ROWS, :].astype(F32)
-        left, right = x[:, :WIDE], x[:, WIDE:]
-        return added(i, packed(left, swap(right)) if LAST[i] * GROUP == first else packed(swap(left), right))
+    def early_a(i):
+        early_terms(4 * i, seen_rows(*PARTS[i]), wo_v, part_bufs[i][0], part_bufs[i][1])
+
+    def early_b(i):
+        first, rows = PARTS[i]
+        h = part_bufs[i][4]
+        h[me] = early_sum(4 * i, seen_rows(first, rows), wo_v, part_bufs[i][1], x_v[first:first + rows, mine].astype(F32))
+        start(4 * i + 1, lambda k: h.at[me], lambda k: h.at[me])
+
+    def early_c(i):
+        first, rows = PARTS[i]
+        h, hidden = part_bufs[i][4:]
+        arrived(4 * i + 1, h.at[:N - 1])
+        hidden_rows(first, rows, lambda c: h[c], hidden)
+        early_terms(4 * i + 2, hidden[...], wd_v, part_bufs[i][2], part_bufs[i][3])
+
+    def early_d(i):
+        first, rows = PARTS[i]
+        block = o_ref.at[first:first + rows, mine]
+        block[...] = early_sum(4 * i + 2, part_bufs[i][5][...], wd_v, part_bufs[i][3], part_bufs[i][4][me].astype(F32))
+        start(4 * i + 3, lambda k: block, lambda k: block)
+
+    def early_size(i, phase):
+        first, rows = PARTS[i]
+        return o_ref.at[first:first + rows, :(N - 1) * HEAD] if phase == 3 else part_bufs[i][1].at[:N - 1]
+
+    def early_e(i):
+        arrived(4 * i + 3, early_size(i, 3))
+
+    def owns(half):
+        a, b, c, d = (me == owner for owner in OWNERS[half])
+        return jnp.logical_or(jnp.logical_or(a, b), jnp.logical_or(c, d))
+
+    def by_role(half, job, ref):
+        @pl.when(owns(half))
+        def _():
+            job(ref(len(OWNERS[half]) - 1))
+
+        @pl.when(jnp.logical_not(owns(half)))
+        def _():
+            job(ref(len(OWNERS[half])))
+
+    def late_terms(half, left, w_v, send, recv):
+        for w, owner in enumerate(OWNERS[half]):
+            for c in range(0, PART, 2 * HEAD):
+                at = w * PART + c
+                send[w, :, c:c + 2 * HEAD] = jnp.dot(left, w_v[:, at:at + 2 * HEAD], preferred_element_type=F32).astype(BF16)
+
+            @pl.when(me != owner)
+            def _():
+                pltpu.make_async_remote_copy(
+                    src_ref=send.at[w], dst_ref=recv.at[other(me, owner)], send_sem=send_sem.at[LATE_AT + 2 * half],
+                    recv_sem=recv_sem.at[LATE_AT + 2 * half], device_id={"tp": owner}, device_id_type=pl.DeviceIdType.MESH).start()
+
+    def late_sum(half, left, w_v, recv, base, block):
+        for w, owner in enumerate(OWNERS[half]):
+            @pl.when(me == owner)
+            def _():
+                total = base(w) + jnp.dot(left, w_v[:, w * PART:(w + 1) * PART], preferred_element_type=F32)
+                arrived(LATE_AT + 2 * half, recv.at[:N - 1])
+                for k in range(1, N):
+                    total += recv[k].astype(F32)
+                block(w)[...] = total.astype(BF16)
+                order = ORDER if half == 0 else sorted(ORDER, key=lambda k: bin((owner ^ k) >> 1).count("1") * 2 + (owner ^ k) % 2)
+                for k in order:
+                    copy(LATE_AT + 1 + 2 * half, k, block(w), block(w)).start()
+
+    def late_a():
+        late_terms(0, seen_rows(EARLY, LATE), wo_v, late_send, late_recv)
+
+    def late_b():
+        late_sum(0, seen_rows(EARLY, LATE), wo_v, late_recv, lambda w: x_v[EARLY:, w * PART:(w + 1) * PART].astype(F32), lambda w: late_h.at[w])
+
+    def late_c():
+        by_role(0, lambda size: arrived(LATE_AT + 1, size), lambda n: late_h.at[:n])
+        per = PART // HEAD
+        hidden_rows(EARLY, LATE, lambda c: late_h[c // per, :, c % per * HEAD:(c % per + 1) * HEAD], late_hidden)
+        late_terms(1, late_hidden[...], wd_v, late_send_m, late_recv_m)
+
+    def late_d():
+        late_sum(1, late_hidden[...], wd_v, late_recv_m, lambda w: late_h[w].astype(F32), lambda w: o_ref.at[EARLY:, w * PART:(w + 1) * PART])
+
+    def late_e():
+        by_role(1, lambda size: arrived(LATE_AT + 3, size), lambda n: o_ref.at[EARLY:, :n * PART])
 
     keys_copy(0).wait()
     score(0)
@@ -252,8 +266,12 @@
             c.wait()
         pl.semaphore_wait(barrier, N - 1)
 
-    stages = {
-        6: (entered,), 7: (lambda: part_a(0),), 9: (lambda: part_b(0),), 13: (lambda: part_a(1),), 14: (lambda: last_a(0),)}
+    def weights():
+        for c in later:
+            c.wait()
+
+    stages = {5: (entered,), 7: (lambda: early_a(0),), 9: (lambda: early_b(0),), 11: (weights, lambda: early_c(0)),
+              13: (lambda: early_a(1), lambda: early_d(0))}
 
     def step(g, _):
         keys_copy(g + 1).wait()
@@ -267,7 +285,7 @@
         def _():
             values_copy(g + 2).start()
 
-        @pl.when(g + 3 == GROUPS)
+        @pl.when(g == WEIGHTS_AT)
         def _():
             for c in later:
                 c.start()
@@ -287,21 +305,26 @@
     lax.fori_loop(0, GROUPS - 1, step, 0)
     values_copy(GROUPS - 1).wait()
     gather(GROUPS - 1)
-    last_a(1)
-    part_b(1)
-    for c in later:
-        c.wait()
-    part_c(0)
-    part_c(1)
-    part_d(0)
-    part_d(1)
-    part_e(0)
-    part_e(1)
+    late_a()
+    early_b(1)
+    late_b()
+    early_c(1)
+    late_c()
+    early_d(1)
+    late_d()
+    early_e(0)
+    early_e(1)
+    late_e()
+
     for i in range(len(PARTS)):
         for phase in range(4):
-            left_here(4 * i + phase, size_of(i, phase))
-    for i in range(len(LAST)):
-        left_here(last_phase(i), last_bufs[i].at[:N - 1])
+            left_here(4 * i + phase, early_size(i, phase))
+    for half, send, recv in ((0, late_send, late_recv), (1, late_send_m, late_recv_m)):
+        by_role(half, lambda size: left_here(LATE_AT + 2 * half, size), lambda n: send.at[:n])
+
+        @pl.when(owns(half))
+        def _():
+            left_here(LATE_AT + 1 + 2 * half, recv.at[:N - 1])
 
 
 def rotary_table():
@@ -327,9 +350,8 @@
                 pltpu.VMEM((FF, D), BF16), pltpu.VMEM((8, HEAD), F32), pltpu.VMEM((BATCH, D), BF16), pltpu.VMEM((GROUPS, ROWS, HEAD), F32),
                 pltpu.VMEM((ROWS, CACHE), F32), pltpu.VMEM((2, ROWS, CACHE), BF16), pltpu.VMEM((GROUPS, ROWS, HEAD), F32),
                 pltpu.VMEM((SLOTS, GROUP, CACHE, HEAD), BF16), pltpu.VMEM((SLOTS, GROUP, CACHE, HEAD), BF16),
-                [[pltpu.VMEM((N, rows, HEAD), BF16) for rows in (direct, direct, count, count, count)] + [pltpu.VMEM((count, FF), BF16)]
-                 for _, count, direct in PARTS],
-                [pltpu.VMEM((N, ROWS, WIDE), BF16) for _ in LAST],
+                [[pltpu.VMEM((N, rows, HEAD), BF16)] * 5 + [pltpu.VMEM((rows, FF), BF16)] for _, rows in PARTS],
+                [pltpu.VMEM((n, LATE, PART), BF16) for n in (4, N, 4, N, 4)] + [pltpu.VMEM((LATE, FF), BF16)],
                 pltpu.SemaphoreType.DMA((9,)), pltpu.SemaphoreType.DMA((SLOTS,)), pltpu.SemaphoreType.DMA((SLOTS,)),
                 pltpu.SemaphoreType.DMA((PHASES,)), pltpu.SemaphoreType.DMA((PHASES,)),
             ],

time: 67 us -> 62.3 us (0.930)
  Pallas kernels: 65.2 us -> 60.5 us
    pallas_call x1, Pallas kernels: 65.2 us -> 60.5 us  [step(): call(x, k_cache.reshape(BATCH, CACHE, HEAD), v_cache.reshape(BATCH, CACHE...]
where the time goes in v3:
time: 62.3 us; the launch traced here: 62.2 us
  Pallas kernels  60.5 us (97%)
  local copies, waits for them, and re-layouts  1.67 us (3%)
    pallas_call x1, Pallas kernels, step(): call(x, k_cache.reshape(BATCH, CACHE, HEAD), v_cache.reshape(BATCH, CACHE...  60.5 us
    unnamed x1, local copies, waits for them, and re-layouts  1.67 us

profile of v3, /device:TPU:0, one launch (start us, length us, event | category | flops | bytes accessed | tf_op | source)
XLA Modules:
  0.0 62.2 jit_solution(14162275765008942509)
XLA Ops:
  0.0 60.5 %decode_layer.1 = bf16[64,2048]{1,0:T(8,128)(2,1)} custom-call(bf16[64,2048]{1,0:T(8,128)(2,1)} %x_hbm.1, bf16[64,4096,128]{2,1,0:T(8,128)(2,1)} %bitcast.k_hbm, bf16[64,4096,128]{2,1,0:T(8,128)(2,1)} %bitcast.1.v_hbm, bf16[16,128]{1,0:T(8,128)(2,1)} %bitcast.4, bf16[2048,128]{1,0:T(8,128)(2,1)} %wq_hbm.1, bf16[128,2048]{1,0:T(8,128)(2,1)} %wo_hbm.1, ...), custom_call_target="tpu_custom_call" | custom-call | tf_op jit(solution)/shard_map/decode_layer/pallas_call | solution.py:361
  60.5 1.7 %copy.13 = bf16[64,2048]{1,0:T(8,128)(2,1)} copy(bf16[64,2048]{1,0:T(8,128)(2,1)} %decode_layer.1) | data formatting | bytes 524288
